TPU v7x, 32 devices: a whole 2x2x4 slice. The times are simulated.
32 devices in a mesh: dp: 2 (over x), ep: 4 (over z), tp: 4 (over y, core).
Axes of the slice: x: 2, y: 2, z: 4, core: 2. Of those that a mesh axis runs over, the one named last changes fastest.
Arguments:
- X: bfloat16 [16384, 1024], P(('dp', 'ep', 'tp')), parts along dimension 0
- idx: int32 [16384, 8], P(('dp', 'ep', 'tp')), parts along dimension 0
- g: float32 [16384, 8], P(('dp', 'ep', 'tp')), parts along dimension 0
- W1: bfloat16 [32, 1024, 512], P('ep', None, 'tp')
- W3: bfloat16 [32, 1024, 512], P('ep', None, 'tp')
- W2: bfloat16 [32, 512, 1024], P('ep', 'tp')
Outputs:
- output: bfloat16 [16384, 1024], P(('dp', 'ep', 'tp')), parts along dimension 0
There are 2 independent parts. A program takes and returns all parts, laid end to end along the dimension named above; an argument that names none is the same for every part.
All inputs are finite; a program needn't handle non-finite values.
Results may differ from a plain program's by a relative error of at most 0.0102037.
Values are sent between devices in bfloat16 or wider.
A program may use at most 1 GiB of HBM per device.

v0:
```python
import jax
import jax.numpy as jnp
from jax import lax
from jax.sharding import PartitionSpec as P

CF = 2


def _route(idx, n_exp, cap):
    ids = idx.reshape(-1)
    oh = (ids[:, None] == jnp.arange(n_exp, dtype=jnp.int32)[None, :]).astype(jnp.int32)
    s = jnp.sum(oh * (jnp.cumsum(oh, axis=0) - 1), axis=1)
    keep = s < cap
    return jnp.where(keep, ids * cap + s, n_exp * cap), keep


def solution(mesh):
    ep, tp = mesh.shape["ep"], mesh.shape["tp"]
    rows = P(("dp", "ep", "tp"), None)

    def local(x, idx, g, w1, w3, w2):
        t_loc, d = x.shape
        top = idx.shape[1]
        el = w1.shape[0]
        n_exp = el * ep
        cap = CF * top * t_loc // n_exp
        dest, keep = _route(idx, n_exp, cap)
        xr = jnp.repeat(x, top, axis=0)
        buf = jnp.zeros((n_exp * cap, d), x.dtype).at[dest].set(xr, mode="drop").reshape(ep, el, cap, d)
        recv = lax.all_to_all(buf, "ep", 0, 0, tiled=True)
        allr = lax.all_gather(recv, "tp", axis=0)
        xe = allr.transpose(2, 0, 1, 3, 4).reshape(el, tp * ep * cap, d)
        h1 = jnp.einsum("erd,edf->erf", xe, w1, preferred_element_type=jnp.float32)
        h3 = jnp.einsum("erd,edf->erf", xe, w3, preferred_element_type=jnp.float32)
        h = (jax.nn.silu(h1) * h3).astype(jnp.bfloat16)
        yp = jnp.einsum("erf,efd->erd", h, w2, preferred_element_type=jnp.float32).astype(jnp.bfloat16)
        yp = yp.reshape(el, tp, ep, cap, d).transpose(1, 2, 0, 3, 4)
        parts = lax.all_to_all(yp, "tp", 0, 0, tiled=True)
        y = jnp.sum(parts.astype(jnp.float32), axis=0).astype(jnp.bfloat16)
        back = lax.all_to_all(y, "ep", 0, 0, tiled=True).reshape(n_exp * cap, d)
        ysel = back[jnp.minimum(dest, n_exp * cap - 1)].astype(jnp.float32).reshape(t_loc, top, d)
        wgt = jnp.where(keep, g.reshape(-1), 0.0).reshape(t_loc, top, 1)
        return jnp.sum(ysel * wgt, axis=1).astype(jnp.bfloat16)

    return jax.shard_map(local, mesh=mesh,
                         in_specs=(rows, rows, rows, P("ep", None, "tp"), P("ep", None, "tp"), P("ep", "tp", None)),
                         out_specs=rows, check_vma=False)
```

profile of v0, /device:TPU:0, one launch (start us, length us, event | category | flops | bytes accessed | tf_op | source)
XLA Modules:
  0.0 2240.6 jit_solution(14913305351969970858)
XLA Ops:
  6.5 0.0 copy-start
  6.5 0.0 all-gather.3.cloned.1.call-start
  6.5 1.0 copy.21
  7.5 0.1 eq.29
  7.7 0.1 eq.25
  7.8 0.7 broadcast_multiply_fusion
  8.6 0.1 fusion.8
  8.6 9.2 reduce-window.6
  17.8 0.8 slice_reduce_fusion
  18.6 0.2 reduce-window.9
  18.8 0.2 add_add_fusion
  19.0 0.1 copy.23
  19.2 0.2 mul.37
  19.3 0.3 fusion.7
  19.7 0.0 copy-start.2
  19.7 0.6 copy-done.2
  20.3 0.6 compare_select_fusion
  21.0 39.1 %scatter_custom_fusion = bf16[8192,1024]{1,0:T(8,128)(2,1)} fusion(s32[4096]{0:T(1024)S(1)} %bitcast.48, bf16[]{:T(256)} %constant.8.clone.1, bf16[512,1024]{1,0:T(8,128)(2,1)} %param.6), kind=kCustom, calls=%fused_computation.7 | custom fusion | bytes 17825794 | tf_op jit(solution)/shard_map/scatter | solution.py:29
  60.1 376.2 %all_to_all.15 = bf16[4,8,256,1024]{3,2,1,0:T(8,128)(2,1)} all-to-all(bf16[4,8,256,1024]{3,2,1,0:T(8,128)(2,1)} %bitcast.43), channel_id=1, replica_groups=mesh['dp'=2,'ep'=4,'tp'=4] {'ep'}, dimensions={0} | all-to-all | bytes 33554432 | tf_op jit(solution)/shard_map/all_to_all | solution.py:30
  436.4 0.0 all-gather.3.cloned.1.call-update
  436.4 400.6 %all-gather.3.cloned.1.call-done = bf16[16,8,256,1024]{3,2,1,0:T(8,128)(2,1)} async-done(((bf16[4,8,256,1024]{3,2,1,0:T(8,128)(2,1)}), bf16[16,8,256,1024]{3,2,1,0:T(8,128)(2,1)}) %all-gather.3.cloned.1.call-update) | async-done | bytes 67108880 | tf_op jit(solution)/shard_map/all_gather | solution.py:31
  837.0 43.3 %copy.24 = bf16[4,4,8,256,1024]{4,3,1,0,2:T(8,128)(2,1)} copy(bf16[4,4,8,256,1024]{4,3,2,1,0:T(8,128)(2,1)} %bitcast.5) | data formatting | bytes 134217728 | tf_op jit(solution)/shard_map/all_gather | solution.py:31
  880.3 31.4 %fusion.10 = f32[8,4096,128]{2,1,0:T(8,128)} fusion(bf16[8,4096,1024]{2,1,0:T(8,128)(2,1)} %bitcast.7, bf16[8,1024,128]{2,1,0:T(8,128)(2,1)} %param.9), kind=kOutput, calls=%fused_computation.28 | convolution fusion | flops 8589934592 | bytes 85983232 | tf_op jit(solution)/shard_map/erd,edf->erf/dot_general | solution.py:33
  911.8 0.0 copy-done
  911.8 70.7 %convolution_convert_fusion = bf16[8,4096,1024]{2,1,0:T(8,128)(2,1)} fusion(bf16[8,128,1024]{2,1,0:T(8,128)(2,1)S(1)} %copy-done, f32[8,4096,128]{2,1,0:T(8,128)} %fusion.10, bf16[8,4096,1024]{2,1,0:T(8,128)(2,1)} %bitcast.7, bf16[8,1024,128]{2,1,0:T(8,128)(2,1)} %param.10), kind=kOutput, calls=%fused_computation.3 | convolution fusion | flops 17238589440 | bytes 155189248 | tf_op jit(solution)/shard_map/erf,efd->erd/dot_general | solution.py:36
  982.5 44.3 %copy.33 = bf16[8,4,4,256,1024]{4,3,2,0,1:T(8,128)(2,1)} copy(bf16[8,4,4,256,1024]{4,3,2,1,0:T(8,128)(2,1)} %bitcast.9) | data formatting | bytes 134217728 | tf_op jit(solution)/shard_map/reshape | solution.py:37
  1026.7 754.4 %all_to_all.16 = bf16[4,4,8,256,1024]{4,3,1,2,0:T(8,128)(2,1)} all-to-all(bf16[4,4,8,256,1024]{4,3,1,2,0:T(8,128)(2,1)} %bitcast.41), channel_id=1, replica_groups=mesh['dp'=2,'ep'=4,'tp'=4] {'tp'}, dimensions={0} | all-to-all | bytes 134217728 | tf_op jit(solution)/shard_map/all_to_all | solution.py:38
  1781.1 30.3 %reduce_sum.34 = bf16[4,8,256,1024]{3,2,0,1:T(8,128)(2,1)} reduce(bf16[4,4,8,256,1024]{4,3,1,2,0:T(8,128)(2,1)} %all_to_all.16, bf16[]{:T(256)} %constant.8.clone.1), dimensions={0}, to_apply=%region_4.5 | reduce | flops 25165824 | bytes 83886080 | tf_op jit(solution)/shard_map/reduce_sum | solution.py:39
  1811.5 13.9 copy.27
  1825.3 0.0 copy-start.3
  1825.3 0.0 copy-start.5
  1825.3 0.0 copy-start.4
  1825.3 7.1 all-to-all-start.2
  1832.5 0.0 copy-done.3
  1832.5 0.2 lt.45
  1832.7 0.0 copy-done.5
  1832.7 0.1 copy.28
  1832.8 0.0 copy-done.4
  1832.9 361.9 %all-to-all-done.2 = bf16[4,8,256,1024]{3,2,1,0:T(8,128)(2,1)} async-done(((bf16[4,8,256,1024]{3,2,1,0:T(8,128)(2,1)}), bf16[4,8,256,1024]{3,2,1,0:T(8,128)(2,1)}, u32[]{:S(2)}, u32[]{:S(2)}) %all-to-all-start.2) | async-done | bytes 16777248 | tf_op jit(solution)/shard_map/all_to_all | solution.py:40
  2194.8 0.0 copy-start.1
  2194.8 29.0 %gather_fusion = bf16[4096,1024]{1,0:T(8,128)(2,1)} fusion(bf16[8192,1024]{1,0:T(8,128)(2,1)} %bitcast.11, s32[4096]{0:T(1024)S(1)} %broadcast_clamp_fusion), kind=kCustom, calls=%fused_computation | custom fusion | bytes 16793600 | tf_op jit(solution)/shard_map/gather | solution.py:41
  2223.8 9.6 fusion
  2233.4 0.0 copy-done.1
  (4 shorter events, 0.1 us)
Async XLA Ops:
  6.5 905.2 %copy-start = (bf16[8,128,1024]{2,1,0:T(8,128)(2,1)S(1)}, bf16[8,128,1024]{2,1,0:T(8,128)(2,1)}, u32[]{:S(2)}) copy-start(bf16[8,128,1024]{2,1,0:T(8,128)(2,1)} %param.11) | copy-start | bytes 6291460
  6.5 830.5 %all-gather.3.cloned.1.call-start = ((), (), s32[]{:S(2)}) async-start(), calls=%async_computation.3 | async-start | bytes 83886080 | tf_op jit(solution)/shard_map/all_gather | solution.py:31
  19.7 0.6 copy-start.2
  1825.3 7.1 copy-start.3
  1825.3 7.3 copy-start.5
  1825.3 7.5 copy-start.4
  1825.3 369.4 %all-to-all-start.2 = ((bf16[4,8,256,1024]{3,2,1,0:T(8,128)(2,1)}), bf16[4,8,256,1024]{3,2,1,0:T(8,128)(2,1)}, u32[]{:S(2)}, u32[]{:S(2)}) async-start(bf16[4,8,256,1024]{3,2,1,0:T(8,128)(2,1)} %copy.27), calls=%async_computation.2 | async-start | bytes 33554432 | tf_op jit(solution)/shard_map/all_to_all | solution.py:40
  2194.8 38.6 %copy-start.1 = (bf16[8,128,1024]{2,1,0:T(8,128)(2,1)S(1)}, bf16[8,128,1024]{2,1,0:T(8,128)(2,1)}, u32[]{:S(2)}) copy-start(bf16[8,128,1024]{2,1,0:T(8,128)(2,1)} %param.11) | copy-start | bytes 6291460
Sparse Core Ops, SparseCore 0:
  436.5 400.4 all-gather.2
where the time goes:
time: 2250 us; the launch traced here: 2240 us
  blocking collectives  1130 us (50%)
  waiting for transfers between devices  763 us (34%)
  local copies, waits for them, and re-layouts  173 us (8%)
  matrix products  102 us (5%)
  other arithmetic  51.4 us (2%)
    all_to_all x1, blocking collectives, local(): parts = lax.all_to_all(yp, 'tp', 0, 0, tiled=True)  754 us
    all_gather x1, waiting for transfers between devices, local(): allr = lax.all_gather(recv, 'tp', axis=0)  401 us
    all_to_all x1, blocking collectives, local(): recv = lax.all_to_all(buf, 'ep', 0, 0, tiled=True)  376 us
    all_to_all x1, waiting for transfers between devices, local(): back = lax.all_to_all(y, 'ep', 0, 0, tiled=True).reshape(n_exp * cap, d)  362 us
    dot_general x1, matrix products, local(): jnp.einsum('erf,efd->erd', h, w2, preferred_element_type=jnp.float32)  70.7 us
  transfers between devices with their start and end apart: 2, of which 2 were waited for; matrix products, arithmetic and copies ran while one was open for 0% of the time, Pallas kernels for 0%

commit v1 on v0

v1 whole, which is shorter than its diff:
```python
import jax
import jax.numpy as jnp
from jax import lax
from jax.sharding import PartitionSpec as P

CF = 2


def _dense_gates(idx, g, n_exp, cap):
    t_loc = idx.shape[0]
    hit = idx[:, :, None] == jnp.arange(n_exp, dtype=jnp.int32)[None, None, :]
    multi = jnp.any(hit, axis=1)
    before = lax.broadcasted_iota(jnp.int32, (t_loc, t_loc), 1) < lax.broadcasted_iota(jnp.int32, (t_loc, t_loc), 0)
    slot = jnp.dot(before.astype(jnp.bfloat16), multi.astype(jnp.bfloat16), preferred_element_type=jnp.float32)
    gate = jnp.sum(jnp.where(hit, g[:, :, None], 0.0), axis=1)
    return jnp.where(slot < cap, gate, 0.0)


def solution(mesh):
    ep, tp = mesh.shape["ep"], mesh.shape["tp"]
    rows = P(("dp", "ep", "tp"), None)

    def local(x, idx, g, w1, w3, w2):
        t_loc, d = x.shape
        top = idx.shape[1]
        el = w1.shape[0]
        n_exp = el * ep
        cap = CF * top * t_loc // n_exp
        gates = _dense_gates(idx, g, n_exp, cap)
        gl = lax.all_to_all(gates.reshape(t_loc, ep, el).transpose(1, 0, 2), "ep", 0, 0, tiled=True).reshape(ep * t_loc, el)
        xa = lax.all_gather(x, "ep", axis=0, tiled=True)
        w13 = lax.all_gather(jnp.concatenate([w1, w3], axis=2), "tp", axis=0)
        w2a = lax.all_gather(w2, "tp", axis=0)
        f = w1.shape[2]
        acc = jnp.zeros((ep * t_loc, d), jnp.float32)
        for e in range(el):
            parts = []
            for s in range(tp):
                ab = jnp.dot(xa, w13[s, e], preferred_element_type=jnp.float32)
                parts.append((jax.nn.silu(ab[:, :f]) * ab[:, f:]).astype(jnp.bfloat16))
            h = jnp.concatenate(parts, axis=1)
            y = jnp.dot(h, w2a[:, e].reshape(tp * f, d), preferred_element_type=jnp.float32)
            acc = acc + gl[:, e:e + 1] * lax.reduce_precision(y, 8, 7)
        return lax.psum_scatter(acc, "ep", scatter_dimension=0, tiled=True).astype(jnp.bfloat16)

    return jax.shard_map(local, mesh=mesh,
                         in_specs=(rows, rows, rows, P("ep", None, "tp"), P("ep", None, "tp"), P("ep", "tp", None)),
                         out_specs=rows, check_vma=False)
```

time: 2250 us -> 561 us (0.25)
  blocking collectives: 1130 us -> 11.9 us
  waiting for transfers between devices: 763 us -> 374 us
  local copies, waits for them, and re-layouts: 173 us -> 7.11 us
  other arithmetic: 51.4 us -> 18 us
  matrix products: 102 us -> 126 us
    all_to_all x2 -> x1, blocking collectives: 1130 us -> 11.9 us  [local(): lax.all_to_all(gates.reshape(t_loc, ep, el).transpose(1, 0, 2), 'ep', 0,...]
    all_to_all x1 -> x0, waiting for transfers between devices: 362 us -> none  [local(): back = lax.all_to_all(y, 'ep', 0, 0, tiled=True).reshape(n_exp * cap, d)]
    all_gather x1 -> x3, waiting for transfers between devices: 401 us -> 228 us  [the longest x1 107 us: local(): w13 = lax.all_gather(jnp.concatenate([w1, w3], axis=2), 'tp', axis=0)]
    reduce_scatter x0 -> x1, waiting for transfers between devices: none -> 144 us  [local(): lax.psum_scatter(acc, 'ep', scatter_dimension=0, tiled=True)]
    reshape x1 -> x0, local copies, waits for them, and re-layouts: 44.3 us -> none  [local(): yp = yp.reshape(el, tp, ep, cap, d).transpose(1, 2, 0, 3, 4)]
    all_gather x1 -> x0, local copies, waits for them, and re-layouts: 43.3 us -> none  [local(): allr = lax.all_gather(recv, 'tp', axis=0)]
    reduce_sum x3 -> x1, other arithmetic: 40.3 us -> 0.06 us  [_dense_gates(): gate = jnp.sum(jnp.where(hit, g[:, :, None], 0.0), axis=1)]
    scatter x1 -> x0, local copies, waits for them, and re-layouts: 39.1 us -> none  [local(): jnp.zeros((n_exp * cap, d), x.dtype).at[dest].set(xr, mode='drop')]
  transfers between devices with their start and end apart: 2 -> 4, of which waited for: 2 -> 4; matrix products, arithmetic and copies ran while one was open for 0% -> 2% of each run, Pallas kernels for 0% -> 0%
where the time goes in v1:
time: 561 us; the launch traced here: 551 us
  waiting for transfers between devices  374 us (67%)
  matrix products  126 us (22%)
  other arithmetic  18 us (3%)
  between operations  13.7 us (2%)
  blocking collectives  11.9 us (2%)
  local copies, waits for them, and re-layouts  7.11 us (1%)
    reduce_scatter x1, waiting for transfers between devices, local(): lax.psum_scatter(acc, 'ep', scatter_dimension=0, tiled=True)  144 us
    all_gather x1, waiting for transfers between devices, local(): w13 = lax.all_gather(jnp.concatenate([w1, w3], axis=2), 'tp', axis=0)  107 us
    all_gather x1, waiting for transfers between devices, local(): xa = lax.all_gather(x, 'ep', axis=0, tiled=True)  76 us
    dot_general x32, matrix products, local(): ab = jnp.dot(xa, w13[s, e], preferred_element_type=jnp.float32)  67.7 us
    dot_general x8, matrix products, local(): jnp.dot(h, w2a[:, e].reshape(tp * f, d), preferred_element_type=jnp.float32)  57.6 us
    all_gather x1, waiting for transfers between devices, local(): w2a = lax.all_gather(w2, 'tp', axis=0)  45 us
    all_to_all x1, blocking collectives, local(): lax.all_to_all(gates.reshape(t_loc, ep, el).transpose(1, 0, 2), 'ep', 0,...  11.9 us
  transfers between devices with their start and end apart: 4, of which 4 were waited for; matrix products, arithmetic and copies ran while one was open for 2% of the time, Pallas kernels for 0%

profile of v1, /device:TPU:0, one launch (start us, length us, event | category | flops | bytes accessed | tf_op | source)
XLA Modules:
  0.0 550.5 jit_solution(14144737395784089853)
XLA Ops:
  6.5 0.7 all-gather.10.cloned.1.call-update
  7.3 0.7 all-gather.6.cloned.1.call-update
  8.1 4.0 pad_maximum_fusion
  13.2 11.9 %all_to_all.5 = f32[4,512,8]{1,2,0:T(8,128)S(1)} all-to-all(f32[4,512,8]{1,2,0:T(8,128)S(1)} %fusion.64), channel_id=1, replica_groups=mesh['dp'=2,'ep'=4,'tp'=4] {'ep'}, dimensions={0} | all-to-all | bytes 131072 | tf_op jit(solution)/shard_map/all_to_all | solution.py:30
  25.2 45.0 %all-gather.10.cloned.1.call-done = bf16[32,128,1024]{2,1,0:T(8,128)(2,1)} async-done(((bf16[8,128,1024]{2,1,0:T(8,128)(2,1)}), bf16[32,128,1024]{2,1,0:T(8,128)(2,1)}) %all-gather.10.cloned.1.call-update) | async-done | bytes 8388624 | tf_op jit(solution)/shard_map/all_gather | solution.py:33
  70.2 5.8 %fusion.106 = (bf16[4,1,128,1024]{3,2,1,0:T(8,128)(2,1)S(1)}, bf16[4,1,128,1024]{3,2,1,0:T(8,128)(2,1)S(1)}, bf16[4,1,128,1024]{3,2,1,0:T(8,128)(2,1)S(1)}, bf16...) fusion(bf16[4,8,128,1024]{3,2,1,0:T(8,128)(2,1)} %bitcast.224), kind=kLoop, calls=%fused_computation.208 | loop fusion | bytes 16777216 | tf_op jit(solution)/shard_map/slice | solution.py:42
  75.9 76.0 %all-gather.6.cloned.1.call-done = bf16[2048,1024]{1,0:T(8,128)(2,1)} async-done(((bf16[512,1024]{1,0:T(8,128)(2,1)}), bf16[2048,1024]{1,0:T(8,128)(2,1)}) %all-gather.6.cloned.1.call-update) | async-done | bytes 4194320 | tf_op jit(solution)/shard_map/all_gather | solution.py:31
  151.9 107.3 %all-gather.8.cloned.1.call-done = bf16[32,1024,256]{2,1,0:T(8,128)(2,1)} async-done(((bf16[8,1024,256]{2,1,0:T(8,128)(2,1)}), bf16[32,1024,256]{2,1,0:T(8,128)(2,1)}) %all-gather.8.cloned.1.call-update) | async-done | bytes 16777232 | tf_op jit(solution)/shard_map/all_gather | solution.py:32
  259.2 3.8 convolution_bitcast_fusion
  263.0 4.4 convolution_bitcast_fusion.1
  267.4 0.6 fusion.65
  268.1 3.7 convolution_bitcast_fusion.2
  271.8 1.3 convolution_bitcast_fusion.3
  273.1 0.6 fusion.67
  273.8 1.3 convolution_bitcast_fusion.4
  275.1 1.3 convolution_bitcast_fusion.5
  276.4 0.6 fusion.69
  277.0 1.3 convolution_bitcast_fusion.6
  278.3 1.3 convolution_bitcast_fusion.7
  279.6 1.1 fusion.71
  280.8 1.3 convolution_bitcast_fusion.8
  282.1 1.3 convolution_bitcast_fusion.9
  283.4 0.6 fusion.73
  284.0 1.3 convolution_bitcast_fusion.10
  285.3 1.3 convolution_bitcast_fusion.11
  286.6 0.6 fusion.75
  287.3 1.3 convolution_bitcast_fusion.12
  288.6 1.3 convolution_bitcast_fusion.13
  289.9 0.6 fusion.77
  290.5 1.3 convolution_bitcast_fusion.14
  291.9 1.3 convolution_bitcast_fusion.15
  293.2 0.8 fusion.79
  294.0 1.3 convolution_bitcast_fusion.16
  295.3 1.3 convolution_bitcast_fusion.17
  296.6 0.6 fusion.81
  297.2 1.3 convolution_bitcast_fusion.18
  298.6 1.3 convolution_bitcast_fusion.19
  299.9 0.6 fusion.83
  300.5 1.3 convolution_bitcast_fusion.20
  301.8 1.3 convolution_bitcast_fusion.21
  303.1 0.6 fusion.85
  303.8 1.3 convolution_bitcast_fusion.22
  305.1 1.3 convolution_bitcast_fusion.23
  306.4 0.9 fusion.87
  307.3 3.5 convolution_bitcast_fusion.24
  310.8 3.5 convolution_bitcast_fusion.25
  314.9 3.5 convolution_bitcast_fusion.26
  318.5 3.5 convolution_bitcast_fusion.27
  322.0 0.6 fusion.91
  322.6 3.5 convolution_bitcast_fusion.28
  326.2 3.5 convolution_bitcast_fusion.29
  329.7 0.6 fusion.93
  330.3 3.5 convolution_bitcast_fusion.30
  333.9 3.9 convolution_bitcast_fusion.31
  339.0 2.4 fusion
  341.5 5.7 %fusion.8 = f32[2048,1024]{1,0:T(8,128)} fusion(bf16[512,1024]{1,0:T(8,128)(2,1)S(1)} %bitcast.231, bf16[2048,128]{0,1:T(8,128)(2,1)S(1)} %get-tuple-element.41, bf16[2048,128]{0,1:T(8,128)(2,1)S(1)} %get-tuple-element.42, bf16[2048,128]{0,1:T(8,128)(2,1)S(1)} %get-tuple-element.43, bf16[2048,128]{0,1:T(8,128)(2,1)S(1)} %get-tuple-element.44), kind=kOutput, calls=%fused_computation.42 | convolution fusion | flops 2155872256 | bytes 11534336 | tf_op jit(solution)/shard_map/dot_general | solution.py:42
  347.1 5.6 %fusion.16 = f32[2048,1024]{1,0:T(8,128)} fusion(bf16[512,1024]{1,0:T(8,128)(2,1)S(1)} %bitcast.230, bf16[2048,128]{0,1:T(8,128)(2,1)S(1)} %get-tuple-element.37, bf16[2048,128]{0,1:T(8,128)(2,1)S(1)} %get-tuple-element.38, bf16[2048,128]{0,1:T(8,128)(2,1)S(1)} %get-tuple-element.39, bf16[2048,128]{0,1:T(8,128)(2,1)S(1)} %get-tuple-element.40), kind=kOutput, calls=%fused_computation.50 | convolution fusion | flops 2155872256 | bytes 11534336 | tf_op jit(solution)/shard_map/dot_general | solution.py:42
  352.8 5.6 %fusion.24 = f32[2048,1024]{1,0:T(8,128)} fusion(bf16[512,1024]{1,0:T(8,128)(2,1)S(1)} %bitcast.229, bf16[2048,128]{0,1:T(8,128)(2,1)S(1)} %get-tuple-element.33, bf16[2048,128]{0,1:T(8,128)(2,1)S(1)} %get-tuple-element.34, bf16[2048,128]{0,1:T(8,128)(2,1)S(1)} %get-tuple-element.35, bf16[2048,128]{0,1:T(8,128)(2,1)S(1)} %get-tuple-element.36), kind=kOutput, calls=%fused_computation.58 | convolution fusion | flops 2155872256 | bytes 11534336 | tf_op jit(solution)/shard_map/dot_general | solution.py:42
  358.4 5.8 %fusion.32 = f32[2048,1024]{1,0:T(8,128)} fusion(bf16[512,1024]{1,0:T(8,128)(2,1)S(1)} %bitcast.228, bf16[2048,128]{0,1:T(8,128)(2,1)S(1)} %get-tuple-element.29, bf16[2048,128]{0,1:T(8,128)(2,1)S(1)} %get-tuple-element.30, bf16[2048,128]{0,1:T(8,128)(2,1)S(1)} %get-tuple-element.31, bf16[2048,128]{0,1:T(8,128)(2,1)S(1)} %get-tuple-element.32), kind=kOutput, calls=%fused_computation.66 | convolution fusion | flops 2155872256 | bytes 11534336 | tf_op jit(solution)/shard_map/dot_general | solution.py:42
  364.3 5.7 %fusion.40 = f32[2048,1024]{1,0:T(8,128)} fusion(bf16[512,1024]{1,0:T(8,128)(2,1)S(1)} %bitcast.227, bf16[2048,128]{0,1:T(8,128)(2,1)S(1)} %get-tuple-element.25, bf16[2048,128]{0,1:T(8,128)(2,1)S(1)} %get-tuple-element.26, bf16[2048,128]{0,1:T(8,128)(2,1)S(1)} %get-tuple-element.27, bf16[2048,128]{0,1:T(8,128)(2,1)S(1)} %get-tuple-element.28), kind=kOutput, calls=%fused_computation.74 | convolution fusion | flops 2155872256 | bytes 11534336 | tf_op jit(solution)/shard_map/dot_general | solution.py:42
  369.9 5.6 %fusion.48 = f32[2048,1024]{1,0:T(8,128)} fusion(bf16[512,1024]{1,0:T(8,128)(2,1)S(1)} %bitcast.226, bf16[2048,128]{0,1:T(8,128)(2,1)S(1)} %get-tuple-element.21, bf16[2048,128]{0,1:T(8,128)(2,1)S(1)} %get-tuple-element.22, bf16[2048,128]{0,1:T(8,128)(2,1)S(1)} %get-tuple-element.23, bf16[2048,128]{0,1:T(8,128)(2,1)S(1)} %get-tuple-element.24), kind=kOutput, calls=%fused_computation.82 | convolution fusion | flops 2155872256 | bytes 11534336 | tf_op jit(solution)/shard_map/dot_general | solution.py:42
  375.6 21.1 %multiply_add_fusion = f32[2048,1024]{1,0:T(8,128)} fusion(f32[2048,1024]{1,0:T(8,128)} %fusion.48, f32[2048,1024]{1,0:T(8,128)} %fusion.40, f32[2048,1024]{1,0:T(8,128)} %fusion.32, f32[2048,1024]{1,0:T(8,128)} %fusion.24, f32[2048,1024]{1,0:T(8,128)} %fusion.16, f32[2048,1024]{1,0:T(8,128)} %fusion.8, f32[2048,1024]{1,0:T(8,128)S(1)} %fusion, ...), kind=kOutput, calls=%fused_computation | convolution fusion | flops 2204106752 | bytes 70320128 | tf_op jit(solution)/shard_map/dot_general | solution.py:42
  396.7 144.3 %reduce-scatter.2.cloned.1.call-done = f32[512,1024]{1,0:T(8,128)} async-done(((f32[2048,1024]{1,0:T(8,128)}), f32[512,1024]{1,0:T(8,128)}) %reduce-scatter.2.cloned.1.call-update) | async-done | bytes 2097168 | tf_op jit(solution)/shard_map/reduce_scatter | solution.py:44
  541.1 2.7 convert_element_type.133
  (32 shorter events, 3.2 us)
Async XLA Ops:
  6.5 1.6 copy-start
  6.5 63.7 %all-gather.10.cloned.1.call-start = ((), (), s32[]{:S(2)}) async-start(), calls=%async_computation.5 | async-start | bytes 10485760 | tf_op jit(solution)/shard_map/all_gather | solution.py:33
  7.3 144.7 %all-gather.6.cloned.1.call-start = ((), (), s32[]{:S(2)}) async-start(), calls=%async_computation.2 | async-start | bytes 5242880 | tf_op jit(solution)/shard_map/all_gather | solution.py:31
  8.0 251.2 %all-gather.8.cloned.1.call-start = ((), (), s32[]{:S(2)}) async-start(), calls=%async_computation.4 | async-start | bytes 20971520 | tf_op jit(solution)/shard_map/all_gather | solution.py:32
  12.1 0.7 copy-start.6
  12.1 0.8 copy-start.7
  12.2 528.9 %reduce-scatter.2.cloned.1.call-start = ((), (), s32[]{:S(2)}) async-start(), calls=%async_computation.3 | async-start | bytes 10485760 | tf_op jit(solution)/shard_map/reduce_scatter | solution.py:44
  259.2 8.9 %copy-start.8 = (bf16[32,1024,256]{2,1,0:T(8,128)(2,1)S(1)}, bf16[32,1024,256]{2,1,0:T(8,128)(2,1)}, u32[]{:S(2)}) copy-start(bf16[32,1024,256]{2,1,0:T(8,128)(2,1)} %all-gather.8.cloned.1.call-done) | copy-start | bytes 50331652
  268.1 3.7 copy-start.9
  337.8 1.2 copy-start.5
  339.0 2.4 copy-start.4
  341.5 5.7 %copy-start.3 = (bf16[4,1,128,1024]{3,2,1,0:T(8,128)(2,1)S(1)}, bf16[4,1,128,1024]{3,2,1,0:T(8,128)(2,1)}, u32[]{:S(2)}) copy-start(bf16[4,1,128,1024]{3,2,1,0:T(8,128)(2,1)} %get-tuple-element.10) | copy-start | bytes 3145732
  347.1 5.6 %copy-start.2 = (bf16[4,1,128,1024]{3,2,1,0:T(8,128)(2,1)S(1)}, bf16[4,1,128,1024]{3,2,1,0:T(8,128)(2,1)}, u32[]{:S(2)}) copy-start(bf16[4,1,128,1024]{3,2,1,0:T(8,128)(2,1)} %get-tuple-element.9) | copy-start | bytes 3145732
  352.8 5.7 %copy-start.1 = (bf16[4,1,128,1024]{3,2,1,0:T(8,128)(2,1)S(1)}, bf16[4,1,128,1024]{3,2,1,0:T(8,128)(2,1)}, u32[]{:S(2)}) copy-start(bf16[4,1,128,1024]{3,2,1,0:T(8,128)(2,1)} %get-tuple-element.8) | copy-start | bytes 3145732
Sparse Core Ops, SparseCore 0:
  8.9 61.2 all-gather.9
  71.8 80.1 all-gather.5
  153.5 105.6 all-gather.7
  396.8 144.1 reduce-scatter.1

commit v2 on v0

v2 whole, which is shorter than its diff:
```python
import functools

import jax
import jax.numpy as jnp
from jax import lax
from jax.experimental import pallas as pl
from jax.experimental.pallas import tpu as pltpu
from jax.sharding import PartitionSpec as P

CF = 2
MESH = pl.DeviceIdType.MESH
NSUB = 4
F32, BF16 = jnp.float32, jnp.bfloat16


def _kernel(cap, x_ref, idx_ref, g_ref, w1_ref, w3_ref, w2_ref, out_ref,
            w13, w2, xall, gsend, gall, gcols, part, from_back, from_fwd,
            ld_x, ld_w, own_s, own_r, y_s, y_r, x_s, x_r, yp_s, yp_r, xp_s, xp_r,
            t_s, t_r, g_s, g_r, r_s, rb_r, rf_r):
    T, D = x_ref.shape
    FL = w1_ref.shape[2]
    TOP = idx_ref.shape[1]
    EL = w1_ref.shape[0]
    KH, TH, TS = D // 2, T // 2, T // NSUB

    xx = lax.axis_index("dp")
    z = lax.axis_index("ep")
    t = lax.axis_index("tp")
    yy, core = t // 2, t % 2
    mate = 2 * yy + 1 - core
    across = 2 * (1 - yy) + core
    to_mate, to_y, to_x = {"tp": mate}, {"tp": across}, {"dp": 1 - xx}
    low = z < 2
    m = jnp.where(low, z, 3 - z)
    fz = jnp.where(low, z + 1, z - 1)
    bz = jnp.where(low, z - 1, z + 1)

    def real(dm):
        return jnp.where(low, dm, 3 - dm)

    def dest(pos):
        return real((m + 1 + pos) % 4)

    def remote(src, dst, ss, rs, dev):
        return pltpu.make_async_remote_copy(src_ref=src, dst_ref=dst, send_sem=ss, recv_sem=rs,
                                            device_id=dev, device_id_type=MESH)

    def piece(e, s, p):
        if p < 2:
            return w13.at[e, s, pl.ds(p * KH, KH)]
        return w2.at[e, pl.ds(pl.multiple_of(s * FL, FL), FL)]

    def load_x():
        return pltpu.make_async_copy(x_ref, xall.at[z], ld_x)

    def load_w(e):
        return (pltpu.make_async_copy(w1_ref.at[e], w13.at[e, t, :, pl.ds(0, FL)], ld_w.at[e, 0]),
                pltpu.make_async_copy(w3_ref.at[e], w13.at[e, t, :, pl.ds(FL, FL)], ld_w.at[e, 1]),
                pltpu.make_async_copy(w2_ref.at[e], w2.at[e, pl.ds(pl.multiple_of(t * FL, FL), FL)], ld_w.at[e, 2]))

    load_x().start()
    for k in range(EL // 2):
        for e in (2 * k + xx, 2 * k + 1 - xx):
            for c in load_w(e):
                c.start()

    barrier = pltpu.get_barrier_semaphore()
    for dev in (to_mate, to_y, to_x, {"ep": (z + 1) % 4}, {"ep": (z + 2) % 4}, {"ep": (z + 3) % 4}):
        pl.semaphore_signal(barrier, inc=1, device_id=dev, device_id_type=MESH)
    pl.semaphore_wait(barrier, 6)

    def own_copy(e, p):
        return remote(piece(e, t, p), piece(e, t, p), own_s.at[e, p], own_r.at[e, p], to_mate)

    def y_copy(k, p):
        return remote(piece(2 * k + xx, t, p), piece(2 * k + xx, t, p), y_s.at[k, p], y_r.at[k, p], to_y)

    def x_copy(k, p):
        r = piece(2 * k + xx, across, p)
        return remote(r, r, x_s.at[k, p], x_r.at[k, p], to_x)

    def yp_copy(k, p):
        r = piece(2 * k + xx, across, p)
        return remote(r, r, yp_s.at[k, p], yp_r.at[k, p], to_mate)

    def xp_copy(k, p):
        r = piece(2 * k + 1 - xx, across, p)
        return remote(r, r, xp_s.at[k, p], xp_r.at[k, p], to_mate)

    def row_copy(src, half, side, hop):
        r = xall.at[src, pl.ds(half * TH, TH)]
        to = {"ep": z + 1 if side == 0 else z - 1}
        return remote(r, r, t_s.at[side, hop, half], t_r.at[src, half], to)

    def rows_wait(src, half):
        r = xall.at[src, pl.ds(half * TH, TH)]
        remote(r, r, t_s.at[0, 0, half], t_r.at[src, half], {"ep": z}).wait_recv()

    def send_own_rows(half):
        @pl.when(z < 3)
        def _():
            row_copy(z, half, 0, 0).start()

        @pl.when(z > 0)
        def _():
            row_copy(z, half, 1, 0).start()

    def first_rows(half):
        @pl.when(m == 0)
        def _():
            rows_wait(dest(0), half)

        @pl.when(m == 1)
        def _():
            rows_wait(z - 1, half)
            row_copy(z - 1, half, 0, 1).start()
            rows_wait(z + 1, half)
            row_copy(z + 1, half, 1, 1).start()

    def second_rows(half):
        rows_wait(dest(1), half)

        @pl.when(z == 1)
        def _():
            row_copy(z + 2, half, 1, 2).start()

        @pl.when(z == 2)
        def _():
            row_copy(z - 2, half, 0, 2).start()

    def third_rows(half):
        @pl.when(m == 0)
        def _():
            rows_wait(dest(2), half)

    load_x().wait()
    send_own_rows(0)
    for k in range(EL // 2):
        e = 2 * k + xx
        for c in load_w(e):
            c.wait()
        for p in range(3):
            y_copy(k, p).start()
        for p in range(3):
            own_copy(e, p).start()

    lane = lax.broadcasted_iota(jnp.int32, (T, 128), 1)
    gate = jnp.zeros((T, 128), F32)
    chosen = jnp.zeros((T, 128), F32)
    for j in range(TOP):
        hit = idx_ref[:, j:j + 1] == lane
        gate = jnp.where(hit, g_ref[:, j:j + 1], gate)
        chosen = jnp.where(hit, 1.0, chosen)
    before = (lax.broadcasted_iota(jnp.int32, (T, T), 1) < lax.broadcasted_iota(jnp.int32, (T, T), 0))
    slot = jnp.dot(before.astype(F32).astype(BF16), chosen.astype(BF16), preferred_element_type=F32)
    gate = jnp.where(slot < float(cap), gate, 0.0)
    gate_t = gate.T
    for r in range(4):
        gsend[r] = gate_t[r * EL:(r + 1) * EL, :]

    def gate_copy(step):
        r = (z + step) % 4
        return remote(gsend.at[r], gall.at[z], g_s.at[step - 1], g_r.at[step - 1], {"ep": r})

    for step in range(1, 4):
        gate_copy(step).start()
    send_own_rows(1)
    for k in range(EL // 2):
        e = 2 * k + 1 - xx
        for c in load_w(e):
            c.wait()
        for p in range(3):
            own_copy(e, p).start()
    part[...] = jnp.zeros_like(part)

    def gate_columns():
        gall[z] = gsend[z]
        for step in range(1, 4):
            gate_copy(step).wait_recv()
        for r in range(4):
            wide = jnp.concatenate([gall[r], jnp.zeros((128 - EL, T), F32)], axis=0)
            gcols[r] = wide.T

    def ready(j):
        k = j // 2
        e = 2 * k + (xx if j % 2 == 0 else 1 - xx)
        for p in range(3):
            own_copy(e, p).wait_recv()
            (yp_copy if j % 2 == 0 else xp_copy)(k, p).wait_recv()

    def unit(j, pos):
        odd = j % 2
        e = (j // 2) * 2 + odd + xx - 2 * odd * xx
        d = dest(pos)
        rows = xall[d]
        hs = []
        for s in range(4):
            ab = jnp.dot(rows, w13[e, s], preferred_element_type=F32)
            hs.append((jax.nn.silu(ab[:, :FL]) * ab[:, FL:]).astype(BF16))
        h = jnp.concatenate(hs, axis=1)
        col = jnp.sum(jnp.where(lane == e, gcols[d], 0.0), axis=1, keepdims=True)
        nb = min(256, D)
        for n in range(D // nb):
            cols = pl.ds(n * nb, nb)
            y = jnp.dot(h, w2[e, :, cols], preferred_element_type=F32).astype(BF16).astype(F32)
            part[d, :, cols] = part[d, :, cols] + col * y

    def units(pos, lo, hi):
        if hi == lo + 1:
            unit(jnp.int32(lo), pos)
            return

        def body(j, c):
            unit(j, pos)
            return c

        lax.fori_loop(lo, hi, body, 0)

    n_slots = 3 * (EL // 2)
    for i in range(n_slots + 1):
        if i < n_slots:
            k, p = divmod(i, 3)
            y_copy(k, p).wait_recv()
            x_copy(k, p).start()
            yp_copy(k, p).start()
        if i >= 1:
            k, p = divmod(i - 1, 3)
            x_copy(k, p).wait_recv()
            xp_copy(k, p).start()
        if i == 2:
            first_rows(0)
        if i == 4:
            first_rows(1)
            gate_columns()
            ready(0)
            ready(1)
            units(0, 0, 2)
        if i == 6:
            second_rows(0)
            ready(2)
            ready(3)
            units(0, 2, 4)
        if i == 8:
            second_rows(1)
            units(1, 0, 2)
        if i == 9:
            units(1, 2, 4)
        if i == 10:
            ready(4)
            ready(5)
            units(1, 4, 6)
        if i == 11:
            ready(6)
            units(1, 6, 7)
    ready(7)
    units(1, 7, 8)

    def chunk(dm, s):
        return part.at[real(dm), pl.ds(pl.multiple_of(s * TS, TS), TS)]

    def sub(ref, i, s):
        return ref.at[i, pl.ds(pl.multiple_of(s * TS, TS), TS)]

    def edge_copy(n, dm, s):
        return remote(chunk(dm, s), sub(from_back, dm - 1, s), r_s.at[n, s], rb_r.at[dm - 1, s], {"ep": fz})

    def inner_copy(n, dm, s):
        return remote(chunk(dm, s), sub(from_fwd, 3 - dm, s), r_s.at[n, s], rf_r.at[3 - dm, s], {"ep": fz})

    def outer_copy(s):
        return remote(chunk(0, s), sub(from_fwd, 0, s), r_s.at[2, s], rf_r.at[0, s], {"ep": bz})

    def back_wait(i, s):
        r = sub(from_back, i, s)
        remote(r, r, r_s.at[0, s], rb_r.at[i, s], {"ep": fz}).wait_recv()

    def fwd_wait(i, s):
        r = sub(from_fwd, i, s)
        remote(r, r, r_s.at[0, s], rf_r.at[i, s], {"ep": fz}).wait_recv()

    def add(dm, ref, i, s):
        here = pl.ds(pl.multiple_of(s * TS, TS), TS)
        d = real(dm)
        part[d, here] = part[d, here] + ref[i, here]

    def pass_on(n, dm, s):
        back_wait(dm - 1, s)
        add(dm, from_back, dm - 1, s)
        inner_copy(n, dm, s).start()

    def pass_out(s):
        fwd_wait(0, s)
        add(0, from_fwd, 0, s)
        outer_copy(s).start()

    def every(fn):
        def body(s, c):
            fn(s)
            return c

        lax.fori_loop(0, NSUB, body, 0)

    @pl.when(m == 0)
    def _():
        every(lambda s: edge_copy(0, 2, s).start())

    for half in range(2):
        third_rows(half)

    def late(g, c):
        @pl.when((m == 1) & (g >= 1))
        def _():
            pass_on(0, 2, g - 1)

        pos = jnp.where(g == 0, 0, jnp.where(g <= 2, 2, 3))
        first = jnp.where(g == 0, 4, 4 * ((g + 1) % 2))

        def body(j, cc):
            unit(first + j, pos)
            return cc

        lax.fori_loop(0, 4, body, 0)

        @pl.when((m == 0) & (g == 2))
        def _():
            every(lambda s: edge_copy(1, 3, s).start())
            every(lambda s: edge_copy(2, 1, s).start())

        return c

    lax.fori_loop(0, NSUB + 1, late, 0)

    @pl.when(m == 1)
    def _():
        pass_on(1, 3, 0)

        def body(s, c):
            pass_on(1, 3, s)
            pass_out(s - 1)
            return c

        lax.fori_loop(1, NSUB, body, 0)
        pass_out(NSUB - 1)

        def last(s):
            here = pl.ds(pl.multiple_of(s * TS, TS), TS)
            fwd_wait(1, s)
            back_wait(0, s)
            out_ref[here] = (part[z, here] + from_back[0, here] + from_fwd[1, here]).astype(out_ref.dtype)

        every(last)

    @pl.when(m == 0)
    def _():
        def last(s):
            here = pl.ds(pl.multiple_of(s * TS, TS), TS)
            fwd_wait(0, s)
            out_ref[here] = (part[z, here] + from_fwd[0, here]).astype(out_ref.dtype)

        every(last)

    for k in range(EL // 2):
        for p in range(3):
            y_copy(k, p).wait_send()
            x_copy(k, p).wait_send()
            yp_copy(k, p).wait_send()
            xp_copy(k, p).wait_send()
            own_copy(2 * k, p).wait_send()
            own_copy(2 * k + 1, p).wait_send()
    for step in range(1, 4):
        gate_copy(step).wait_send()
    for half in range(2):
        @pl.when(z < 3)
        def _():
            row_copy(z, half, 0, 0).wait_send()

        @pl.when(z > 0)
        def _():
            row_copy(z, half, 1, 0).wait_send()

        @pl.when(m == 1)
        def _():
            row_copy(z - 1, half, 0, 1).wait_send()
            row_copy(z + 1, half, 1, 1).wait_send()

        @pl.when(z == 1)
        def _():
            row_copy(z + 2, half, 1, 2).wait_send()

        @pl.when(z == 2)
        def _():
            row_copy(z - 2, half, 0, 2).wait_send()

    @pl.when(m == 0)
    def _():
        for n, dm in ((0, 2), (1, 3), (2, 1)):
            every(lambda s: edge_copy(n, dm, s).wait_send())

    @pl.when(m == 1)
    def _():
        for n, dm in ((0, 2), (1, 3)):
            every(lambda s: inner_copy(n, dm, s).wait_send())
        every(lambda s: outer_copy(s).wait_send())


def solution(mesh):
    ep, tp = mesh.shape["ep"], mesh.shape["tp"]
    rows = P(("dp", "ep", "tp"), None)

    def local(x, idx, g, w1, w3, w2):
        T, D = x.shape
        top = idx.shape[1]
        EL, _, FL = w1.shape
        cap = CF * top * T // (EL * ep)
        any_spec = pl.BlockSpec(memory_space=pl.ANY)
        vmem_spec = pl.BlockSpec(memory_space=pltpu.VMEM)
        dma = pltpu.SemaphoreType.DMA
        half_e = EL // 2
        return pl.pallas_call(
            functools.partial(_kernel, cap),
            name="moe",
            out_shape=jax.ShapeDtypeStruct((T, D), x.dtype),
            in_specs=[any_spec, vmem_spec, vmem_spec, any_spec, any_spec, any_spec],
            out_specs=vmem_spec,
            scratch_shapes=[
                pltpu.VMEM((EL, tp, D, 2 * FL), BF16),
                pltpu.VMEM((EL, tp * FL, D), BF16),
                pltpu.VMEM((ep, T, D), BF16),
                pltpu.VMEM((ep, EL, T), F32),
                pltpu.VMEM((ep, EL, T), F32),
                pltpu.VMEM((ep, T, 128), F32),
                pltpu.VMEM((ep, T, D), F32),
                pltpu.VMEM((3, T, D), F32),
                pltpu.VMEM((2, T, D), F32),
                dma, dma((EL, 3)),
                dma((EL, 3)), dma((EL, 3)),
                dma((half_e, 3)), dma((half_e, 3)),
                dma((half_e, 3)), dma((half_e, 3)),
                dma((half_e, 3)), dma((half_e, 3)),
                dma((half_e, 3)), dma((half_e, 3)),
                dma((2, 3, 2)), dma((4, 2)),
                dma((3,)), dma((3,)),
                dma((3, NSUB)), dma((3, NSUB)), dma((2, NSUB)),
            ],
            compiler_params=pltpu.CompilerParams(collective_id=0, has_side_effects=True,
                                                 vmem_limit_bytes=67_043_328),
        )(x, idx, g, w1, w3, w2)

    return jax.shard_map(local, mesh=mesh,
                         in_specs=(rows, rows, rows, P("ep", None, "tp"), P("ep", None, "tp"), P("ep", "tp", None)),
                         out_specs=rows, check_vma=False)
```

time: 2250 us -> 231 us (0.10)
  blocking collectives: 1130 us -> 0 us
  waiting for transfers between devices: 763 us -> 0 us
  Pallas kernels: 0 us -> 225 us
  local copies, waits for them, and re-layouts: 173 us -> 5.38 us
  matrix products: 102 us -> 0 us
  other arithmetic: 51.4 us -> 0 us
    all_to_all x2 -> x0, blocking collectives: 1130 us -> none  [the longest x1 754 us: local(): parts = lax.all_to_all(yp, 'tp', 0, 0, tiled=True)]
    all_gather x1 -> x0, waiting for transfers between devices: 401 us -> none  [local(): allr = lax.all_gather(recv, 'tp', axis=0)]
    all_to_all x1 -> x0, waiting for transfers between devices: 362 us -> none  [local(): back = lax.all_to_all(y, 'ep', 0, 0, tiled=True).reshape(n_exp * cap, d)]
    pallas_call x0 -> x1, Pallas kernels: none -> 225 us  [local(): pl.pallas_call(functools.partial(_kernel, cap), name='moe', out_shape=jax...]
    dot_general x2 -> x0, matrix products: 102 us -> none  [the longest x1 70.7 us: local(): jnp.einsum('erf,efd->erd', h, w2, preferred_element_type=jnp.float32)]
    reshape x1 -> x0, local copies, waits for them, and re-layouts: 44.3 us -> none  [local(): yp = yp.reshape(el, tp, ep, cap, d).transpose(1, 2, 0, 3, 4)]
    all_gather x1 -> x0, local copies, waits for them, and re-layouts: 43.3 us -> none  [local(): allr = lax.all_gather(recv, 'tp', axis=0)]
    reduce_sum x3 -> x0, other arithmetic: 40.3 us -> none  [the longest x1 30.3 us: local(): y = jnp.sum(parts.astype(jnp.float32), axis=0).astype(jnp.bfloat16)]
  transfers between devices with their start and end apart: 2 -> 0, of which waited for: 2 -> 0; matrix products, arithmetic and copies ran while one was open for 0% -> 0% of each run, Pallas kernels for 0% -> 0%
where the time goes in v2:
time: 231 us; the launch traced here: 230 us
  Pallas kernels  225 us (97%)
  local copies, waits for them, and re-layouts  5.38 us (2%)
    pallas_call x1, Pallas kernels, local(): pl.pallas_call(functools.partial(_kernel, cap), name='moe', out_shape=jax...  225 us
    unnamed x3, local copies, waits for them, and re-layouts  5.38 us

profile of v2, /device:TPU:0, one launch (start us, length us, event | category | flops | bytes accessed | tf_op | source)
XLA Modules:
  0.0 230.4 jit_solution(13377293706514602175)
XLA Ops:
  0.0 1.6 copy.7.idx_ref
  1.6 1.6 copy.8.g_ref
  3.1 225.0 %moe.1 = bf16[512,1024]{1,0:T(8,128)(2,1)} custom-call(bf16[512,1024]{1,0:T(8,128)(2,1)} %x_ref.1, s32[512,8]{1,0:T(8,128)} %copy.7.idx_ref, f32[512,8]{1,0:T(8,128)} %copy.8.g_ref, bf16[8,1024,128]{2,1,0:T(8,128)(2,1)} %w1_ref.1, bf16[8,1024,128]{2,1,0:T(8,128)(2,1)} %w3_ref.1, bf16[8,128,1024]{2,1,0:T(8,128)(2,1)} %w2_ref.1), custom_call_target="tpu_custom_call" | custom-call | tf_op jit(solution)/shard_map/moe/pallas_call | solution.py:419
  228.1 2.3 copy.10

commit v3 on v2

--- a/solution.py
+++ b/solution.py
@@ -9,17 +9,17 @@
 
 CF = 2
 MESH = pl.DeviceIdType.MESH
-NSUB = 4
+NSUB = 8
 F32, BF16 = jnp.float32, jnp.bfloat16
 
 
 def _kernel(cap, x_ref, idx_ref, g_ref, w1_ref, w3_ref, w2_ref, out_ref,
-            w13, w2, xall, gsend, gall, gcols, part, from_back, from_fwd,
+            w13, w2, xall, gsend, gall, gcols, part, from_back, from_fwd, done,
             ld_x, ld_w, own_s, own_r, y_s, y_r, x_s, x_r, yp_s, yp_r, xp_s, xp_r,
-            t_s, t_r, g_s, g_r, r_s, rb_r, rf_r):
+            t_s, t_r, g_s, g_r, r_s, rb_r, rf_r, d_s, d_r):
     T, D = x_ref.shape
     FL = w1_ref.shape[2]
-    TOP = idx_ref.shape[1]
+    TOP = idx_ref.shape[0]
     EL = w1_ref.shape[0]
     KH, TH, TS = D // 2, T // 2, T // NSUB
 
@@ -144,19 +144,19 @@
         for p in range(3):
             own_copy(e, p).start()
 
-    lane = lax.broadcasted_iota(jnp.int32, (T, 128), 1)
-    gate = jnp.zeros((T, 128), F32)
-    chosen = jnp.zeros((T, 128), F32)
+    NE = gsend.shape[0] * EL
+    expert = lax.broadcasted_iota(jnp.int32, (NE, T), 0)
+    gate = jnp.zeros((NE, T), F32)
+    chosen = jnp.zeros((NE, T), F32)
     for j in range(TOP):
-        hit = idx_ref[:, j:j + 1] == lane
-        gate = jnp.where(hit, g_ref[:, j:j + 1], gate)
+        hit = idx_ref[j:j + 1, :] == expert
+        gate = jnp.where(hit, g_ref[j:j + 1, :], gate)
         chosen = jnp.where(hit, 1.0, chosen)
-    before = (lax.broadcasted_iota(jnp.int32, (T, T), 1) < lax.broadcasted_iota(jnp.int32, (T, T), 0))
-    slot = jnp.dot(before.astype(F32).astype(BF16), chosen.astype(BF16), preferred_element_type=F32)
+    before = (lax.broadcasted_iota(jnp.int32, (T, T), 0) < lax.broadcasted_iota(jnp.int32, (T, T), 1))
+    slot = jnp.dot(chosen.astype(BF16), before.astype(F32).astype(BF16), preferred_element_type=F32)
     gate = jnp.where(slot < float(cap), gate, 0.0)
-    gate_t = gate.T
     for r in range(4):
-        gsend[r] = gate_t[r * EL:(r + 1) * EL, :]
+        gsend[r] = gate[r * EL:(r + 1) * EL, :]
 
     def gate_copy(step):
         r = (z + step) % 4
@@ -173,6 +173,8 @@
             own_copy(e, p).start()
     part[...] = jnp.zeros_like(part)
 
+    lane = lax.broadcasted_iota(jnp.int32, (T, 128), 1)
+
     def gate_columns():
         gall[z] = gsend[z]
         for step in range(1, 4):
@@ -188,10 +190,10 @@
             own_copy(e, p).wait_recv()
             (yp_copy if j % 2 == 0 else xp_copy)(k, p).wait_recv()
 
-    def unit(j, pos):
+    def unit(j, dm):
         odd = j % 2
         e = (j // 2) * 2 + odd + xx - 2 * odd * xx
-        d = dest(pos)
+        d = real(dm)
         rows = xall[d]
         hs = []
         for s in range(4):
@@ -205,13 +207,9 @@
             y = jnp.dot(h, w2[e, :, cols], preferred_element_type=F32).astype(BF16).astype(F32)
             part[d, :, cols] = part[d, :, cols] + col * y
 
-    def units(pos, lo, hi):
-        if hi == lo + 1:
-            unit(jnp.int32(lo), pos)
-            return
-
+    def units(dm, lo, hi):
         def body(j, c):
-            unit(j, pos)
+            unit(j, dm)
             return c
 
         lax.fori_loop(lo, hi, body, 0)
@@ -234,128 +232,127 @@
             gate_columns()
             ready(0)
             ready(1)
+            units(1, 0, 2)
+        if i == 5:
             units(0, 0, 2)
         if i == 6:
             second_rows(0)
             ready(2)
             ready(3)
+            units(1, 2, 4)
+        if i == 7:
             units(0, 2, 4)
         if i == 8:
             second_rows(1)
-            units(1, 0, 2)
+            units(2, 0, 2)
         if i == 9:
-            units(1, 2, 4)
+            units(2, 2, 4)
         if i == 10:
             ready(4)
             ready(5)
-            units(1, 4, 6)
+            units(2, 4, 6)
         if i == 11:
             ready(6)
-            units(1, 6, 7)
+            units(2, 6, 7)
     ready(7)
-    units(1, 7, 8)
-
-    def chunk(dm, s):
-        return part.at[real(dm), pl.ds(pl.multiple_of(s * TS, TS), TS)]
-
-    def sub(ref, i, s):
-        return ref.at[i, pl.ds(pl.multiple_of(s * TS, TS), TS)]
-
-    def edge_copy(n, dm, s):
-        return remote(chunk(dm, s), sub(from_back, dm - 1, s), r_s.at[n, s], rb_r.at[dm - 1, s], {"ep": fz})
-
-    def inner_copy(n, dm, s):
-        return remote(chunk(dm, s), sub(from_fwd, 3 - dm, s), r_s.at[n, s], rf_r.at[3 - dm, s], {"ep": fz})
-
-    def outer_copy(s):
-        return remote(chunk(0, s), sub(from_fwd, 0, s), r_s.at[2, s], rf_r.at[0, s], {"ep": bz})
-
-    def back_wait(i, s):
-        r = sub(from_back, i, s)
-        remote(r, r, r_s.at[0, s], rb_r.at[i, s], {"ep": fz}).wait_recv()
-
-    def fwd_wait(i, s):
-        r = sub(from_fwd, i, s)
-        remote(r, r, r_s.at[0, s], rf_r.at[i, s], {"ep": fz}).wait_recv()
-
-    def add(dm, ref, i, s):
-        here = pl.ds(pl.multiple_of(s * TS, TS), TS)
-        d = real(dm)
-        part[d, here] = part[d, here] + ref[i, here]
-
-    def pass_on(n, dm, s):
-        back_wait(dm - 1, s)
-        add(dm, from_back, dm - 1, s)
-        inner_copy(n, dm, s).start()
-
-    def pass_out(s):
-        fwd_wait(0, s)
-        add(0, from_fwd, 0, s)
-        outer_copy(s).start()
-
-    def every(fn):
+    units(2, 7, 8)
+
+    def at(s):
+        return pl.ds(pl.multiple_of(s * TS, TS), TS)
+
+    def edge_copy(n, s):
+        dm = 2 + n
+        return remote(part.at[real(dm), at(s)], from_back.at[n, at(s)], r_s.at[n, s], rb_r.at[n, s], {"ep": fz})
+
+    def fwd_copy(n, s):
+        dm = 2 + n
+        return remote(part.at[real(dm), at(s)], from_fwd.at[1 - n, at(s)], r_s.at[n, s], rf_r.at[1 - n, s], {"ep": fz})
+
+    def bwd_copy(n, s):
+        dm = 1 - n
+        return remote(part.at[real(dm), at(s)], from_fwd.at[dm, at(s)], r_s.at[2 + n, s], rf_r.at[dm, s], {"ep": bz})
+
+    def done_copy(s):
+        return remote(done.at[at(s)], out_ref.at[at(s)], d_s.at[s], d_r.at[s], {"ep": fz})
+
+    def fwd_wait(dm, s):
+        r = from_fwd.at[dm, at(s)]
+        remote(r, r, r_s.at[0, s], rf_r.at[dm, s], {"ep": fz}).wait_recv()
+
+    def pass_fwd(i):
+        n, s = i // NSUB, i % NSUB
+        edge_copy(n, s).wait_recv()
+        d = real(2 + n)
+        part[d, at(s)] = part[d, at(s)] + from_back[n, at(s)]
+        fwd_copy(n, s).start()
+
+    def pass_bwd(i):
+        n, s = i // NSUB, i % NSUB
+        fwd_wait(1 - n, s)
+        d = real(1 - n)
+        part[d, at(s)] = part[d, at(s)] + from_fwd[1 - n, at(s)]
+        bwd_copy(n, s).start()
+
+    def both(i):
+        pass_fwd(i)
+        pass_bwd(i - 1)
+
+    def loop(lo, hi, fn):
         def body(s, c):
             fn(s)
             return c
 
-        lax.fori_loop(0, NSUB, body, 0)
+        lax.fori_loop(lo, hi, body, 0)
+
+    def every(fn):
+        loop(0, NSUB, fn)
 
     @pl.when(m == 0)
     def _():
-        every(lambda s: edge_copy(0, 2, s).start())
+        every(lambda s: edge_copy(0, s).start())
 
     for half in range(2):
         third_rows(half)
 
     def late(g, c):
-        @pl.when((m == 1) & (g >= 1))
-        def _():
-            pass_on(0, 2, g - 1)
-
-        pos = jnp.where(g == 0, 0, jnp.where(g <= 2, 2, 3))
-        first = jnp.where(g == 0, 4, 4 * ((g + 1) % 2))
-
-        def body(j, cc):
-            unit(first + j, pos)
-            return cc
-
-        lax.fori_loop(0, 4, body, 0)
+        @pl.when((m == 1) & (g == 1))
+        def _():
+            pass_fwd(0)
+
+        @pl.when((m == 1) & (g >= 2))
+        def _():
+            loop(2 * g - 3, 2 * g - 1, both)
+
+        dm = jnp.where(g == 0, 1, jnp.where(g == 3, 0, 3))
+        first = jnp.where(g == 1, 0, 4)
+        loop(first, first + 4, lambda j: unit(j, dm))
 
         @pl.when((m == 0) & (g == 2))
         def _():
-            every(lambda s: edge_copy(1, 3, s).start())
-            every(lambda s: edge_copy(2, 1, s).start())
+            every(lambda s: edge_copy(1, s).start())
 
         return c
 
-    lax.fori_loop(0, NSUB + 1, late, 0)
+    lax.fori_loop(0, 4, late, 0)
 
     @pl.when(m == 1)
     def _():
-        pass_on(1, 3, 0)
-
-        def body(s, c):
-            pass_on(1, 3, s)
-            pass_out(s - 1)
-            return c
-
-        lax.fori_loop(1, NSUB, body, 0)
-        pass_out(NSUB - 1)
-
-        def last(s):
-            here = pl.ds(pl.multiple_of(s * TS, TS), TS)
-            fwd_wait(1, s)
-            back_wait(0, s)
-            out_ref[here] = (part[z, here] + from_back[0, here] + from_fwd[1, here]).astype(out_ref.dtype)
-
-        every(last)
+        loop(5, 2 * NSUB, both)
+        pass_bwd(2 * NSUB - 1)
+        every(lambda s: done_copy(s).wait_recv())
 
     @pl.when(m == 0)
     def _():
+        def finish(s):
+            fwd_wait(1, s)
+            done[at(s)] = (part[real(1), at(s)] + from_fwd[1, at(s)]).astype(done.dtype)
+            done_copy(s).start()
+
+        every(finish)
+
         def last(s):
-            here = pl.ds(pl.multiple_of(s * TS, TS), TS)
             fwd_wait(0, s)
-            out_ref[here] = (part[z, here] + from_fwd[0, here]).astype(out_ref.dtype)
+            out_ref[at(s)] = (part[z, at(s)] + from_fwd[0, at(s)]).astype(out_ref.dtype)
 
         every(last)
 
@@ -393,14 +390,15 @@
 
     @pl.when(m == 0)
     def _():
-        for n, dm in ((0, 2), (1, 3), (2, 1)):
-            every(lambda s: edge_copy(n, dm, s).wait_send())
+        for n in range(2):
+            every(lambda s: edge_copy(n, s).wait_send())
+        every(lambda s: done_copy(s).wait_send())
 
     @pl.when(m == 1)
     def _():
-        for n, dm in ((0, 2), (1, 3)):
-            every(lambda s: inner_copy(n, dm, s).wait_send())
-        every(lambda s: outer_copy(s).wait_send())
+        for n in range(2):
+            every(lambda s: fwd_copy(n, s).wait_send())
+            every(lambda s: bwd_copy(n, s).wait_send())
 
 
 def solution(mesh):
@@ -430,8 +428,9 @@
                 pltpu.VMEM((ep, EL, T), F32),
                 pltpu.VMEM((ep, T, 128), F32),
                 pltpu.VMEM((ep, T, D), F32),
-                pltpu.VMEM((3, T, D), F32),
                 pltpu.VMEM((2, T, D), F32),
+                pltpu.VMEM((2, T, D), F32),
+                pltpu.VMEM((T, D), BF16),
                 dma, dma((EL, 3)),
                 dma((EL, 3)), dma((EL, 3)),
                 dma((half_e, 3)), dma((half_e, 3)),
@@ -440,11 +439,12 @@
                 dma((half_e, 3)), dma((half_e, 3)),
                 dma((2, 3, 2)), dma((4, 2)),
                 dma((3,)), dma((3,)),
-                dma((3, NSUB)), dma((3, NSUB)), dma((2, NSUB)),
+                dma((4, NSUB)), dma((2, NSUB)), dma((2, NSUB)),
+                dma((NSUB,)), dma((NSUB,)),
             ],
             compiler_params=pltpu.CompilerParams(collective_id=0, has_side_effects=True,
                                                  vmem_limit_bytes=67_043_328),
-        )(x, idx, g, w1, w3, w2)
+        )(x, idx.T, g.T, w1, w3, w2)
 
     return jax.shard_map(local, mesh=mesh,
                          in_specs=(rows, rows, rows, P("ep", None, "tp"), P("ep", None, "tp"), P("ep", "tp", None)),

time: 231 us -> 208 us (0.900)
  Pallas kernels: 225 us -> 204 us
  local copies, waits for them, and re-layouts: 5.38 us -> 2.26 us
    pallas_call x1, Pallas kernels: 225 us -> 204 us  [local(): pl.pallas_call(functools.partial(_kernel, cap), name='moe', out_shape=jax...]
    unnamed x3 -> x1, local copies, waits for them, and re-layouts: 5.38 us -> 2.26 us
where the time goes in v3:
time: 208 us; the launch traced here: 206 us
  Pallas kernels  204 us (98%)
  local copies, waits for them, and re-layouts  2.26 us (1%)
    pallas_call x1, Pallas kernels, local(): pl.pallas_call(functools.partial(_kernel, cap), name='moe', out_shape=jax...  204 us

profile of v3, /device:TPU:0, one launch (start us, length us, event | category | flops | bytes accessed | tf_op | source)
XLA Modules:
  0.0 206.4 jit_solution(5316385596946868853)
XLA Ops:
  0.0 204.2 %moe.1 = bf16[512,1024]{1,0:T(8,128)(2,1)} custom-call(bf16[512,1024]{1,0:T(8,128)(2,1)} %x_ref.1, s32[8,512]{1,0:T(8,128)} %bitcast.2, f32[8,512]{1,0:T(8,128)} %bitcast.3, bf16[8,1024,128]{2,1,0:T(8,128)(2,1)} %w1_ref.1, bf16[8,1024,128]{2,1,0:T(8,128)(2,1)} %w3_ref.1, bf16[8,128,1024]{2,1,0:T(8,128)(2,1)} %w2_ref.1), custom_call_target="tpu_custom_call" | custom-call | tf_op jit(solution)/shard_map/moe/pallas_call | solution.py:417
  204.2 2.3 %copy.8 = bf16[512,1024]{1,0:T(8,128)(2,1)} copy(bf16[512,1024]{1,0:T(8,128)(2,1)} %moe.1) | data formatting | bytes 2097152

commit v4 on v3

--- a/solution.py
+++ b/solution.py
@@ -14,8 +14,8 @@
 
 
 def _kernel(cap, x_ref, idx_ref, g_ref, w1_ref, w3_ref, w2_ref, out_ref,
-            w13, w2, xall, gsend, gall, gcols, part, from_back, from_fwd, done,
-            ld_x, ld_w, own_s, own_r, y_s, y_r, x_s, x_r, yp_s, yp_r, xp_s, xp_r,
+            idx_v, g_v, w13, w2, xall, gsend, gall, gcols, part, from_back, from_fwd, done,
+            ld_i, ld_x, ld_w, own_s, own_r, y_s, y_r, x_s, x_r, yp_s, yp_r, xp_s, xp_r,
             t_s, t_r, g_s, g_r, r_s, rb_r, rf_r, d_s, d_r):
     T, D = x_ref.shape
     FL = w1_ref.shape[2]
@@ -50,6 +50,9 @@
             return w13.at[e, s, pl.ds(p * KH, KH)]
         return w2.at[e, pl.ds(pl.multiple_of(s * FL, FL), FL)]
 
+    def load_i():
+        return (pltpu.make_async_copy(idx_ref, idx_v, ld_i.at[0]), pltpu.make_async_copy(g_ref, g_v, ld_i.at[1]))
+
     def load_x():
         return pltpu.make_async_copy(x_ref, xall.at[z], ld_x)
 
@@ -59,7 +62,12 @@
                 pltpu.make_async_copy(w2_ref.at[e], w2.at[e, pl.ds(pl.multiple_of(t * FL, FL), FL)], ld_w.at[e, 2]))
 
     load_x().start()
-    for k in range(EL // 2):
+    for e in (xx, 1 - xx):
+        for c in load_w(e):
+            c.start()
+    for c in load_i():
+        c.start()
+    for k in range(1, EL // 2):
         for e in (2 * k + xx, 2 * k + 1 - xx):
             for c in load_w(e):
                 c.start()
@@ -69,15 +77,26 @@
         pl.semaphore_signal(barrier, inc=1, device_id=dev, device_id_type=MESH)
     pl.semaphore_wait(barrier, 6)
 
+    LAST = (EL // 2 - 1, 5)
+
+    def small(e, s, q):
+        if q < 4:
+            return w13.at[e, s, pl.ds(q * (KH // 2), KH // 2)]
+        return w2.at[e, pl.ds(pl.multiple_of(s * FL + (q - 4) * (FL // 2), FL // 2), FL // 2)]
+
     def own_copy(e, p):
         return remote(piece(e, t, p), piece(e, t, p), own_s.at[e, p], own_r.at[e, p], to_mate)
 
-    def y_copy(k, p):
-        return remote(piece(2 * k + xx, t, p), piece(2 * k + xx, t, p), y_s.at[k, p], y_r.at[k, p], to_y)
-
-    def x_copy(k, p):
-        r = piece(2 * k + xx, across, p)
-        return remote(r, r, x_s.at[k, p], x_r.at[k, p], to_x)
+    def y_copy(k, q):
+        r = small(2 * k + xx, t, q)
+        return remote(r, r, y_s.at[k, q], y_r.at[k, q], to_y)
+
+    def x_copy(k, q):
+        if (k, q) == LAST:
+            r = small(2 * k + 1 - xx, t, q)
+            return remote(r, r, x_s.at[k, q], x_r.at[k, q], to_y)
+        r = small(2 * k + xx, across, q)
+        return remote(r, r, x_s.at[k, q], x_r.at[k, q], to_x)
 
     def yp_copy(k, p):
         r = piece(2 * k + xx, across, p)
@@ -139,18 +158,20 @@
         e = 2 * k + xx
         for c in load_w(e):
             c.wait()
-        for p in range(3):
-            y_copy(k, p).start()
+        for q in range(6):
+            y_copy(k, q).start()
         for p in range(3):
             own_copy(e, p).start()
 
+    for c in load_i():
+        c.wait()
     NE = gsend.shape[0] * EL
     expert = lax.broadcasted_iota(jnp.int32, (NE, T), 0)
     gate = jnp.zeros((NE, T), F32)
     chosen = jnp.zeros((NE, T), F32)
     for j in range(TOP):
-        hit = idx_ref[j:j + 1, :] == expert
-        gate = jnp.where(hit, g_ref[j:j + 1, :], gate)
+        hit = idx_v[j:j + 1, :] == expert
+        gate = jnp.where(hit, g_v[j:j + 1, :], gate)
         chosen = jnp.where(hit, 1.0, chosen)
     before = (lax.broadcasted_iota(jnp.int32, (T, T), 0) < lax.broadcasted_iota(jnp.int32, (T, T), 1))
     slot = jnp.dot(chosen.astype(BF16), before.astype(F32).astype(BF16), preferred_element_type=F32)
@@ -171,6 +192,7 @@
             c.wait()
         for p in range(3):
             own_copy(e, p).start()
+    x_copy(*LAST).start()
     part[...] = jnp.zeros_like(part)
 
     lane = lax.broadcasted_iota(jnp.int32, (T, 128), 1)
@@ -207,55 +229,41 @@
             y = jnp.dot(h, w2[e, :, cols], preferred_element_type=F32).astype(BF16).astype(F32)
             part[d, :, cols] = part[d, :, cols] + col * y
 
-    def units(dm, lo, hi):
-        def body(j, c):
-            unit(j, dm)
-            return c
-
-        lax.fori_loop(lo, hi, body, 0)
-
-    n_slots = 3 * (EL // 2)
+    plan = {9: (1, 0), 10: (1, 1), 11: (0, 0), 12: (0, 1), 13: (1, 2), 14: (1, 3), 15: (0, 2), 16: (0, 3),
+            17: (2, 0), 18: (2, 1), 19: (2, 2), 20: (2, 3), 21: (2, 4), 22: (2, 5), 24: (2, 6)}
+    first_use = {9: 0, 10: 1, 13: 2, 14: 3, 21: 4, 22: 5, 24: 6}
+    n_slots = 6 * (EL // 2)
     for i in range(n_slots + 1):
         if i < n_slots:
-            k, p = divmod(i, 3)
-            y_copy(k, p).wait_recv()
-            x_copy(k, p).start()
-            yp_copy(k, p).start()
+            k, q = divmod(i, 6)
+            y_copy(k, q).wait_recv()
+            if (k, q) != LAST:
+                x_copy(k, q).start()
+            if q % 2 == 1:
+                yp_copy(k, q // 2).start()
         if i >= 1:
-            k, p = divmod(i - 1, 3)
-            x_copy(k, p).wait_recv()
-            xp_copy(k, p).start()
-        if i == 2:
+            k, q = divmod(i - 1, 6)
+            if (k, q) != LAST:
+                x_copy(k, q).wait_recv()
+                if q % 2 == 1:
+                    xp_copy(k, q // 2).start()
+        if i == 5:
             first_rows(0)
-        if i == 4:
+        if i == 8:
             first_rows(1)
             gate_columns()
-            ready(0)
-            ready(1)
-            units(1, 0, 2)
-        if i == 5:
-            units(0, 0, 2)
-        if i == 6:
+        if i == 13:
             second_rows(0)
-            ready(2)
-            ready(3)
-            units(1, 2, 4)
-        if i == 7:
-            units(0, 2, 4)
-        if i == 8:
+        if i == 17:
             second_rows(1)
-            units(2, 0, 2)
-        if i == 9:
-            units(2, 2, 4)
-        if i == 10:
-            ready(4)
-            ready(5)
-            units(2, 4, 6)
-        if i == 11:
-            ready(6)
-            units(2, 6, 7)
+        if i in first_use:
+            ready(first_use[i])
+        if i in plan:
+            unit(jnp.int32(plan[i][1]), plan[i][0])
+    x_copy(*LAST).wait_recv()
+    xp_copy(LAST[0], 2).start()
     ready(7)
-    units(2, 7, 8)
+    unit(jnp.int32(7), 2)
 
     def at(s):
         return pl.ds(pl.multiple_of(s * TS, TS), TS)
@@ -357,9 +365,10 @@
         every(last)
 
     for k in range(EL // 2):
+        for q in range(6):
+            y_copy(k, q).wait_send()
+            x_copy(k, q).wait_send()
         for p in range(3):
-            y_copy(k, p).wait_send()
-            x_copy(k, p).wait_send()
             yp_copy(k, p).wait_send()
             xp_copy(k, p).wait_send()
             own_copy(2 * k, p).wait_send()
@@ -410,7 +419,7 @@
         top = idx.shape[1]
         EL, _, FL = w1.shape
         cap = CF * top * T // (EL * ep)
-        any_spec = pl.BlockSpec(memory_space=pl.ANY)
+        hbm_spec = pl.BlockSpec(memory_space=pltpu.MemorySpace.HBM)
         vmem_spec = pl.BlockSpec(memory_space=pltpu.VMEM)
         dma = pltpu.SemaphoreType.DMA
         half_e = EL // 2
@@ -418,9 +427,11 @@
             functools.partial(_kernel, cap),
             name="moe",
             out_shape=jax.ShapeDtypeStruct((T, D), x.dtype),
-            in_specs=[any_spec, vmem_spec, vmem_spec, any_spec, any_spec, any_spec],
+            in_specs=[hbm_spec] * 6,
             out_specs=vmem_spec,
             scratch_shapes=[
+                pltpu.VMEM((top, T), jnp.int32),
+                pltpu.VMEM((top, T), F32),
                 pltpu.VMEM((EL, tp, D, 2 * FL), BF16),
                 pltpu.VMEM((EL, tp * FL, D), BF16),
                 pltpu.VMEM((ep, T, D), BF16),
@@ -431,10 +442,10 @@
                 pltpu.VMEM((2, T, D), F32),
                 pltpu.VMEM((2, T, D), F32),
                 pltpu.VMEM((T, D), BF16),
-                dma, dma((EL, 3)),
+                dma((2,)), dma, dma((EL, 3)),
                 dma((EL, 3)), dma((EL, 3)),
-                dma((half_e, 3)), dma((half_e, 3)),
-                dma((half_e, 3)), dma((half_e, 3)),
+                dma((half_e, 6)), dma((half_e, 6)),
+                dma((half_e, 6)), dma((half_e, 6)),
                 dma((half_e, 3)), dma((half_e, 3)),
                 dma((half_e, 3)), dma((half_e, 3)),
                 dma((2, 3, 2)), dma((4, 2)),
@@ -443,7 +454,7 @@
                 dma((NSUB,)), dma((NSUB,)),
             ],
             compiler_params=pltpu.CompilerParams(collective_id=0, has_side_effects=True,
-                                                 vmem_limit_bytes=67_043_328),
+                                                 vmem_limit_bytes=52 << 20),
         )(x, idx.T, g.T, w1, w3, w2)
 
     return jax.shard_map(local, mesh=mesh,

time: 208 us -> 209 us (level)
  no operation moved by 1% of the time
where the time goes in v4:
time: 209 us; the launch traced here: 207 us
  Pallas kernels  205 us (98%)
  local copies, waits for them, and re-layouts  2.41 us (1%)
    pallas_call x1, Pallas kernels, local(): pl.pallas_call(functools.partial(_kernel, cap), name='moe', out_shape=jax...  205 us

profile of v4, /device:TPU:0, one launch (start us, length us, event | category | flops | bytes accessed | tf_op | source)
XLA Modules:
  0.0 207.4 jit_solution(3471419575703534851)
XLA Ops:
  0.0 0.0 copy-start
  0.0 0.7 copy-done
  0.7 0.0 copy-start.1
  0.7 0.7 copy-done.1
  1.4 205.0 %moe.1 = bf16[512,1024]{1,0:T(8,128)(2,1)S(1)} custom-call(bf16[512,1024]{1,0:T(8,128)(2,1)} %x_ref.1, s32[8,512]{1,0:T(8,128)S(1)} %bitcast.2, f32[8,512]{1,0:T(8,128)S(1)} %bitcast.3, bf16[8,1024,128]{2,1,0:T(8,128)(2,1)} %w1_ref.1, bf16[8,1024,128]{2,1,0:T(8,128)(2,1)} %w3_ref.1, bf16[8,128,1024]{2,1,0:T(8,128)(2,1)} %w2_ref.1), custom_call_target="tpu_custom_call" | custom-call | tf_op jit(solution)/shard_map/moe/pallas_call | solution.py:426
  206.4 1.0 copy.8
Async XLA Ops:
  0.0 0.7 copy-start
  0.7 0.7 copy-start.1

commit v5 on v3

--- a/solution.py
+++ b/solution.py
@@ -233,15 +233,11 @@
             ready(0)
             ready(1)
             units(1, 0, 2)
-        if i == 5:
-            units(0, 0, 2)
         if i == 6:
             second_rows(0)
             ready(2)
             ready(3)
             units(1, 2, 4)
-        if i == 7:
-            units(0, 2, 4)
         if i == 8:
             second_rows(1)
             units(2, 0, 2)
@@ -324,8 +320,8 @@
             loop(2 * g - 3, 2 * g - 1, both)
 
         dm = jnp.where(g == 0, 1, jnp.where(g == 3, 0, 3))
-        first = jnp.where(g == 1, 0, 4)
-        loop(first, first + 4, lambda j: unit(j, dm))
+        first = jnp.where((g == 1) | (g == 3), 0, 4)
+        loop(first, jnp.where(g == 1, 4, 8), lambda j: unit(j, dm))
 
         @pl.when((m == 0) & (g == 2))
         def _():
@@ -443,7 +439,7 @@
                 dma((NSUB,)), dma((NSUB,)),
             ],
             compiler_params=pltpu.CompilerParams(collective_id=0, has_side_effects=True,
-                                                 vmem_limit_bytes=67_043_328),
+                                                 vmem_limit_bytes=52 << 20),
         )(x, idx.T, g.T, w1, w3, w2)
 
     return jax.shard_map(local, mesh=mesh,

time: 208 us -> 213 us (1.024)
  Pallas kernels: 204 us -> 210 us
    pallas_call x1, Pallas kernels: 204 us -> 210 us  [local(): pl.pallas_call(functools.partial(_kernel, cap), name='moe', out_shape=jax...]
where the time goes in v5:
time: 213 us; the launch traced here: 212 us
  Pallas kernels  210 us (99%)
  local copies, waits for them, and re-layouts  2.41 us (1%)
    pallas_call x1, Pallas kernels, local(): pl.pallas_call(functools.partial(_kernel, cap), name='moe', out_shape=jax...  210 us

profile of v5, /device:TPU:0, one launch (start us, length us, event | category | flops | bytes accessed | tf_op | source)
XLA Modules:
  0.0 212.1 jit_solution(11250816000409166150)
XLA Ops:
  0.0 0.0 copy-start
  0.0 0.7 copy-done
  0.7 0.0 copy-start.1
  0.7 0.7 copy-done.1
  1.4 209.6 %moe.1 = bf16[512,1024]{1,0:T(8,128)(2,1)S(1)} custom-call(bf16[512,1024]{1,0:T(8,128)(2,1)} %x_ref.1, s32[8,512]{1,0:T(8,128)S(1)} %bitcast.2, f32[8,512]{1,0:T(8,128)S(1)} %bitcast.3, bf16[8,1024,128]{2,1,0:T(8,128)(2,1)} %w1_ref.1, bf16[8,1024,128]{2,1,0:T(8,128)(2,1)} %w3_ref.1, bf16[8,128,1024]{2,1,0:T(8,128)(2,1)} %w2_ref.1), custom_call_target="tpu_custom_call" | custom-call | tf_op jit(solution)/shard_map/moe/pallas_call | solution.py:413
  211.1 1.0 copy.8
Async XLA Ops:
  0.0 0.7 copy-start
  0.7 0.7 copy-start.1
